TPU v7x, 256 devices: a whole 4x4x8 slice. The times are simulated.
256 devices in a mesh: gz: 64 (over x, y_lo, z), gx: 4 (over y_hi, core).
Axes of the slice: x: 4, y: 4 (y_hi: 2, y_lo: 2; y = y_hi * 2 + y_lo), z: 8, core: 2. Of those that a mesh axis runs over, the one named last changes fastest.
Arguments:
- noisy_volume: float32 [256, 512, 512], P('gz', 'gx'), may hold values from -3 to 3, as said below
- tv_weight: float32 [256, 512, 512], P('gz', 'gx'), may hold values from 0.05 to 0.5
Outputs:
- denoised: float32 [256, 512, 512], P('gz', 'gx')
- gap_values: float32 [4], replicated
- step_values: float32 [4], replicated
Inputs may be any that keep to these rules, and one draw needn't show every extreme that they name: `noisy_volume`: voxel intensities.
All inputs are finite; a program needn't handle non-finite values.
Results may differ from a plain program's by a relative error of at most 0.0001.
Values sent between devices are 32-bit elements; how exact they have to be, the bound alone decides.
A program may use at most 64 MiB of HBM per device.

v0:
```python
import functools

import jax
import jax.numpy as jnp
from jax import lax
from jax.sharding import Mesh
from jax.sharding import PartitionSpec as P

ITERS = 4
GZ = ("gz_0", "gz_1", "gz_2")
GX = ("gx_0", "gx_1")
GZ_GX = ("gz_0", "gz_1", "gz_2", "gx_0", "gx_1")


primal_step = 0.28
dual_step = 0.28


def shifted_2(value, axis, steps):
    count = lax.axis_size(axis)
    initial, last = (max(0, -steps), min(count, count - steps))
    return lax.ppermute(value, axis, [(source, source + steps) for source in range(initial, last)])


def one_axis_at_a_time(array, axes):
    return functools.reduce(lax.psum, axes, array)


def gradient(volume, next_plane, next_row, keep_plane, keep_row):
    along_z = (jnp.concatenate([volume[1:], next_plane], axis=0) - volume) * keep_plane
    along_x = (jnp.concatenate([volume[:, 1:], next_row], axis=1) - volume) * keep_row
    along_y = jnp.concatenate(
        [volume[:, :, 1:] - volume[:, :, :-1], jnp.zeros_like(volume[:, :, :1])], axis=2
    )
    return (along_z, along_x, along_y)


def divergence(dual_field, prev_plane, prev_row):
    dual_z, dual_x, dual_y = dual_field
    back_z = dual_z - jnp.concatenate([prev_plane, dual_z[:-1]], axis=0)
    back_x = dual_x - jnp.concatenate([prev_row, dual_x[:, :-1]], axis=1)
    back_y = dual_y - jnp.concatenate([jnp.zeros_like(dual_y[:, :, :1]), dual_y[:, :, :-1]], axis=2)
    return back_z + back_x + back_y


def shards(noisy_volume, tv_weight):
    planes_dev, rows_dev, cols_dev = noisy_volume.shape
    cell_count = planes_dev * rows_dev * cols_dev * lax.axis_size(GZ) * lax.axis_size(GX)
    last_slab = lax.axis_index(GZ) == lax.axis_size(GZ) - 1
    last_block = lax.axis_index(GX) == lax.axis_size(GX) - 1
    plane_ids = lax.iota(jnp.int32, planes_dev)
    row_ids = lax.iota(jnp.int32, rows_dev)
    keep_plane = (
        jnp.where(jnp.logical_or(plane_ids < planes_dev - 1, jnp.logical_not(last_slab)), 1.0, 0.0)
        .astype(jnp.float32)
        .reshape(planes_dev, 1, 1)
    )
    keep_row = (
        jnp.where(jnp.logical_or(row_ids < rows_dev - 1, jnp.logical_not(last_block)), 1.0, 0.0)
        .astype(jnp.float32)
        .reshape(1, rows_dev, 1)
    )
    primal = noisy_volume
    extrapolated = noisy_volume
    zeros_field = jnp.zeros_like(noisy_volume)
    dual_field = (zeros_field, zeros_field, zeros_field)
    grad_primal = None
    gap_list = []
    step_list = []
    for iteration in range(ITERS):
        next_planes = shifted_2((primal[:1], extrapolated[:1]), GZ, -1)
        next_rows = shifted_2((primal[:, :1], extrapolated[:, :1]), GX, -1)
        grad_primal = gradient(primal, next_planes[0], next_rows[0], keep_plane, keep_row)
        grad_extra = gradient(extrapolated, next_planes[1], next_rows[1], keep_plane, keep_row)
        proposed = tuple(
            (
                dual_part + dual_step * grad_part
                for dual_part, grad_part in zip(dual_field, grad_extra)
            )
        )
        magnitude = jnp.sqrt(
            proposed[0] * proposed[0] + proposed[1] * proposed[1] + proposed[2] * proposed[2]
        )
        shrink = tv_weight / jnp.maximum(tv_weight, magnitude)
        dual_field = tuple((part * shrink for part in proposed))
        prev_plane = shifted_2(dual_field[0][-1:], GZ, 1)
        prev_row = shifted_2(dual_field[1][:, -1:], GX, 1)
        spread = divergence(dual_field, prev_plane, prev_row)
        updated = (primal + primal_step * (spread + noisy_volume)) / (1.0 + primal_step)
        total_var = jnp.sqrt(
            grad_primal[0] * grad_primal[0]
            + grad_primal[1] * grad_primal[1]
            + grad_primal[2] * grad_primal[2]
        )
        misfit = primal - noisy_volume
        shifted = noisy_volume + spread
        gap_terms = (
            0.5 * misfit * misfit
            + tv_weight * total_var
            - 0.5 * noisy_volume * noisy_volume
            + 0.5 * shifted * shifted
        )
        change = updated - primal
        gap_part = jnp.sum(gap_terms)
        step_part = jnp.sum(change * change)
        gap_list.append(gap_part)
        step_list.append(step_part)
        extrapolated = 2.0 * updated - primal
        primal = updated
    gap_total, step_total = (
        one_axis_at_a_time(jnp.stack(gap_list), GZ_GX),
        one_axis_at_a_time(jnp.stack(step_list), GZ_GX),
    )
    gap_values = gap_total / cell_count
    step_values = jnp.sqrt(step_total / cell_count)
    return (primal, gap_values, step_values)


def solution(mesh):
    torus = Mesh(mesh.devices.reshape(4, 2, 8, 2, 2), ("gz_0", "gz_1", "gz_2", "gx_0", "gx_1"))
    placed = (P(GZ, GX, None), P(GZ, GX, None))
    return jax.shard_map(
        shards, mesh=torus, in_specs=placed, out_specs=(P(GZ, GX, None), P(), P()), check_vma=False
    )
```

profile of v0, /device:TPU:1, one launch (start us, length us, event | category | flops | bytes accessed | tf_op | source)
XLA Modules:
  0.0 167.8 jit_solution(9475778811589459721)
XLA Ops:
  1.6 1.3 collective-permute-start
  3.8 5.2 %collective-permute-start.1 = (f32[4,1,512]{2,1,0:T(1,128)S(1)}, f32[4,1,512]{2,1,0:T(1,128)S(1)}, u32[]{:S(2)}, u32[]{:S(2)}) collective-permute-start(f32[4,1,512]{2,1,0:T(1,128)S(1)} %slice.195), channel_id=1, source_target_pairs={{1,0},{2,1},{3,2},{5,4},{6,5},{7,6},{9,8},{10,9},{11,10},{13,12},{... | collective-permute-start | bytes 24584 | tf_op jit(solution)/shard_map/ppermute | solution.py:22
  9.0 1.9 %slice_subtract_fusion.6 = f32[4,128,511]{2,1,0:T(8,128)S(1)} fusion(f32[4,128,512]{2,1,0:T(8,128)} %param.2), kind=kLoop, calls=%fused_computation.127 | loop fusion | flops 261632 | bytes 3139584 | tf_op jit(solution)/shard_map/sub | solution.py:33
  13.8 4.3 %collective-permute-start.2 = (f32[1,128,512]{2,1,0:T(8,128)S(1)}, f32[1,128,512]{2,1,0:T(8,128)S(1)}, u32[]{:S(2)}, u32[]{:S(2)}) collective-permute-start(f32[1,128,512]{2,1,0:T(8,128)S(1)} %slice.254), channel_id=1, source_target_pairs={{0,4},{4,8},{8,12},{12,16},{16,20},{20,24},{24,28},{28,32},{32,36}... | collective-permute-start | bytes 786440 | tf_op jit(solution)/shard_map/ppermute | solution.py:22
  18.1 5.2 %collective-permute-start.3 = (f32[4,1,512]{2,1,0:T(1,128)S(1)}, f32[4,1,512]{2,1,0:T(1,128)S(1)}, u32[]{:S(2)}, u32[]{:S(2)}) collective-permute-start(f32[4,1,512]{2,1,0:T(1,128)S(1)} %slice.256), channel_id=1, source_target_pairs={{0,1},{1,2},{2,3},{4,5},{5,6},{6,7},{8,9},{9,10},{10,11},{12,13},{... | collective-permute-start | bytes 24584 | tf_op jit(solution)/shard_map/ppermute | solution.py:22
  25.1 1.3 collective-permute-start.4
  26.4 2.4 %collective-permute-start.5 = (f32[4,1,512]{2,1,0:T(1,128)S(1)}, f32[4,1,512]{2,1,0:T(1,128)S(1)}, u32[]{:S(2)}, u32[]{:S(2)}) collective-permute-start(f32[4,1,512]{2,1,0:T(1,128)S(1)} %slice.262), channel_id=1, source_target_pairs={{1,0},{2,1},{3,2},{5,4},{6,5},{7,6},{9,8},{10,9},{11,10},{13,12},{... | collective-permute-start | bytes 24584 | tf_op jit(solution)/shard_map/ppermute | solution.py:22
  29.6 1.3 collective-permute-start.16
  30.9 1.9 %collective-permute-start.17 = (f32[4,1,512]{2,1,0:T(1,128)S(1)}, f32[4,1,512]{2,1,0:T(1,128)S(1)}, u32[]{:S(2)}, u32[]{:S(2)}) collective-permute-start(f32[4,1,512]{2,1,0:T(1,128)S(1)} %slice.295), channel_id=1, source_target_pairs={{1,0},{2,1},{3,2},{5,4},{6,5},{7,6},{9,8},{10,9},{11,10},{13,12},{... | collective-permute-start | bytes 24584 | tf_op jit(solution)/shard_map/ppermute | solution.py:22
  35.9 5.8 %collective-permute-start.6 = (f32[1,128,512]{2,1,0:T(8,128)S(1)}, f32[1,128,512]{2,1,0:T(8,128)S(1)}, u32[]{:S(2)}, u32[]{:S(2)}) collective-permute-start(f32[1,128,512]{2,1,0:T(8,128)S(1)} %slice.265), channel_id=1, source_target_pairs={{0,4},{4,8},{8,12},{12,16},{16,20},{20,24},{24,28},{28,32},{32,36}... | collective-permute-start | bytes 786440 | tf_op jit(solution)/shard_map/ppermute | solution.py:22
  41.7 3.9 %collective-permute-start.7 = (f32[4,1,512]{2,1,0:T(1,128)S(1)}, f32[4,1,512]{2,1,0:T(1,128)S(1)}, u32[]{:S(2)}, u32[]{:S(2)}) collective-permute-start(f32[4,1,512]{2,1,0:T(1,128)S(1)} %slice.267), channel_id=1, source_target_pairs={{0,1},{1,2},{2,3},{4,5},{5,6},{6,7},{8,9},{9,10},{10,11},{12,13},{... | collective-permute-start | bytes 24584 | tf_op jit(solution)/shard_map/ppermute | solution.py:22
  47.2 5.0 %fusion.3 = (f32[]{:T(128)}, f32[]{:T(128)}, f32[]{:T(128)}, f32[]{:T(128)}, f32[4,128,512]{2,1,0:T(8,128)S(1)}, /*index=5*/f32[4,128,512]{2,1,0:T(8,128)S(1)}) fusion(f32[4,128,512]{2,1,0:T(8,128)S(1)} %get-tuple-element.39, f32[4,128,512]{2,1,0:T(8,128)S(1)} %copy-done.4, f32[4,128,512]{2,1,0:T(8,128)S(1)} %copy-done, ...), kind=kLoop, calls=%fused_computation.16 | loop fusion | flops 15728636 | bytes 18868768 | tf_op jit(solution)/shard_map/reduce_sum | solution.py:104
  52.5 1.3 collective-permute-start.8
  53.8 2.8 %collective-permute-start.9 = (f32[4,1,512]{2,1,0:T(1,128)S(1)}, f32[4,1,512]{2,1,0:T(1,128)S(1)}, u32[]{:S(2)}, u32[]{:S(2)}) collective-permute-start(f32[4,1,512]{2,1,0:T(1,128)S(1)} %slice.273), channel_id=1, source_target_pairs={{1,0},{2,1},{3,2},{5,4},{6,5},{7,6},{9,8},{10,9},{11,10},{13,12},{... | collective-permute-start | bytes 24584 | tf_op jit(solution)/shard_map/ppermute | solution.py:22
  57.2 3.1 %collective-permute-done.9 = f32[4,1,512]{2,1,0:T(1,128)S(1)} collective-permute-done((f32[4,1,512]{2,1,0:T(1,128)S(1)}, f32[4,1,512]{2,1,0:T(1,128)S(1)}, u32[]{:S(2)}, u32[]{:S(2)}) %collective-permute-start.9) | collective-permute-done | bytes 8224 | tf_op jit(solution)/shard_map/ppermute | solution.py:22
  60.3 1.8 %collective-permute-done.8 = f32[1,128,512]{2,1,0:T(8,128)S(1)} collective-permute-done((f32[1,128,512]{2,1,0:T(8,128)S(1)}, f32[1,128,512]{2,1,0:T(8,128)S(1)}, u32[]{:S(2)}, u32[]{:S(2)}) %collective-permute-start.8) | collective-permute-done | bytes 262176 | tf_op jit(solution)/shard_map/ppermute | solution.py:22
  63.7 4.8 %collective-permute-start.10 = (f32[1,128,512]{2,1,0:T(8,128)S(1)}, f32[1,128,512]{2,1,0:T(8,128)S(1)}, u32[]{:S(2)}, u32[]{:S(2)}) collective-permute-start(f32[1,128,512]{2,1,0:T(8,128)S(1)} %slice.276), channel_id=1, source_target_pairs={{0,4},{4,8},{8,12},{12,16},{16,20},{20,24},{24,28},{28,32},{32,36}... | collective-permute-start | bytes 786440 | tf_op jit(solution)/shard_map/ppermute | solution.py:22
  68.5 5.1 %collective-permute-start.11 = (f32[4,1,512]{2,1,0:T(1,128)S(1)}, f32[4,1,512]{2,1,0:T(1,128)S(1)}, u32[]{:S(2)}, u32[]{:S(2)}) collective-permute-start(f32[4,1,512]{2,1,0:T(1,128)S(1)} %slice.278), channel_id=1, source_target_pairs={{0,1},{1,2},{2,3},{4,5},{5,6},{6,7},{8,9},{9,10},{10,11},{12,13},{... | collective-permute-start | bytes 24584 | tf_op jit(solution)/shard_map/ppermute | solution.py:22
  75.5 1.9 %collective-permute-start.19 = (f32[4,1,512]{2,1,0:T(1,128)S(1)}, f32[4,1,512]{2,1,0:T(1,128)S(1)}, u32[]{:S(2)}, u32[]{:S(2)}) collective-permute-start(f32[4,1,512]{2,1,0:T(1,128)S(1)} %slice.301), channel_id=1, source_target_pairs={{1,0},{2,1},{3,2},{5,4},{6,5},{7,6},{9,8},{10,9},{11,10},{13,12},{... | collective-permute-start | bytes 24584 | tf_op jit(solution)/shard_map/ppermute | solution.py:22
  79.9 1.9 %collective-permute-start.13 = (f32[4,1,512]{2,1,0:T(1,128)S(1)}, f32[4,1,512]{2,1,0:T(1,128)S(1)}, u32[]{:S(2)}, u32[]{:S(2)}) collective-permute-start(f32[4,1,512]{2,1,0:T(1,128)S(1)} %slice.284), channel_id=1, source_target_pairs={{1,0},{2,1},{3,2},{5,4},{6,5},{7,6},{9,8},{10,9},{11,10},{13,12},{... | collective-permute-start | bytes 24584 | tf_op jit(solution)/shard_map/ppermute | solution.py:22
  84.0 2.4 %collective-permute-done.13 = f32[4,1,512]{2,1,0:T(1,128)S(1)} collective-permute-done((f32[4,1,512]{2,1,0:T(1,128)S(1)}, f32[4,1,512]{2,1,0:T(1,128)S(1)}, u32[]{:S(2)}, u32[]{:S(2)}) %collective-permute-start.13) | collective-permute-done | bytes 8224 | tf_op jit(solution)/shard_map/ppermute | solution.py:22
  86.4 1.9 %collective-permute-start.21 = (f32[4,1,512]{2,1,0:T(1,128)S(1)}, f32[4,1,512]{2,1,0:T(1,128)S(1)}, u32[]{:S(2)}, u32[]{:S(2)}) collective-permute-start(f32[4,1,512]{2,1,0:T(1,128)S(1)} %slice.307), channel_id=1, source_target_pairs={{1,0},{2,1},{3,2},{5,4},{6,5},{7,6},{9,8},{10,9},{11,10},{13,12},{... | collective-permute-start | bytes 24584 | tf_op jit(solution)/shard_map/ppermute | solution.py:22
  88.3 2.1 %collective-permute-done.12 = f32[1,128,512]{2,1,0:T(8,128)S(1)} collective-permute-done((f32[1,128,512]{2,1,0:T(8,128)S(1)}, f32[1,128,512]{2,1,0:T(8,128)S(1)}, u32[]{:S(2)}, u32[]{:S(2)}) %collective-permute-start.12) | collective-permute-done | bytes 262176 | tf_op jit(solution)/shard_map/ppermute | solution.py:22
  92.1 5.3 %collective-permute-start.14 = (f32[1,128,512]{2,1,0:T(8,128)S(1)}, f32[1,128,512]{2,1,0:T(8,128)S(1)}, u32[]{:S(2)}, u32[]{:S(2)}) collective-permute-start(f32[1,128,512]{2,1,0:T(8,128)S(1)} %slice.287), channel_id=1, source_target_pairs={{0,4},{4,8},{8,12},{12,16},{16,20},{20,24},{24,28},{28,32},{32,36}... | collective-permute-start | bytes 786440 | tf_op jit(solution)/shard_map/ppermute | solution.py:22
  97.4 3.6 %collective-permute-start.15 = (f32[4,1,512]{2,1,0:T(1,128)S(1)}, f32[4,1,512]{2,1,0:T(1,128)S(1)}, u32[]{:S(2)}, u32[]{:S(2)}) collective-permute-start(f32[4,1,512]{2,1,0:T(1,128)S(1)} %slice.289), channel_id=1, source_target_pairs={{0,1},{1,2},{2,3},{4,5},{5,6},{6,7},{8,9},{9,10},{10,11},{12,13},{... | collective-permute-start | bytes 24584 | tf_op jit(solution)/shard_map/ppermute | solution.py:22
  102.7 5.7 %fusion.11 = (f32[]{:T(128)}, f32[]{:T(128)}, f32[]{:T(128)}, f32[]{:T(128)}, f32[4,128,512]{2,1,0:T(8,128)}) fusion(f32[4,128,512]{2,1,0:T(8,128)S(1)} %get-tuple-element.29, f32[4,128,512]{2,1,0:T(8,128)S(1)} %copy-done.4, f32[4,128,512]{2,1,0:T(8,128)S(1)} %get-tuple-element.21, f32[1,128,512]{2,1,0:T(8,128)S(1)} %collective-permute-done.18, ...), kind=kLoop, calls=%fused_computation.24 | loop fusion | flops 15990780 | bytes 18868768 | tf_op jit(solution)/shard_map/reduce_sum | solution.py:104
  108.4 5.1 %pad_maximum_fusion = (f32[4]{0:T(128)S(1)}, f32[4]{0:T(128)S(1)}) fusion(f32[1]{0:T(128)} %bitcast.3, f32[1]{0:T(128)} %bitcast.2, f32[1]{0:T(128)} %bitcast.1, f32[1]{0:T(128)} %bitcast, f32[1]{0:T(128)} %bitcast.7, f32[1]{0:T(128)} %bitcast.6, f32[1]{0:T(128)} %bitcast.5, f32[1]{0:T(128)} %bitcast.4), kind=kLoop, calls=%fused_computation.139 | loop fusion | flops 24 | bytes 64 | tf_op jit(solution)/shard_map/stack | solution.py:111
  113.4 21.7 %all-reduce.12 = (f32[4]{0:T(128)S(1)}, f32[4]{0:T(128)S(1)}) all-reduce(f32[4]{0:T(128)S(1)} %get-tuple-element.50, f32[4]{0:T(128)S(1)} %get-tuple-element.51), channel_id=1, replica_groups=mesh['gz_0'=4,'gz_1'=2,'gz_2'=8,'gx_0'=2,'gx_1'=2] {'gz_0'}, use_global_device_ids=true, to_apply=%region_4.5 | all-reduce | flops 8 | bytes 64 | tf_op jit(solution)/shard_map/psum | solution.py:26
  135.1 3.8 %all-reduce.15 = (f32[4]{0:T(128)S(1)}, f32[4]{0:T(128)S(1)}) all-reduce(f32[4]{0:T(128)S(1)} %get-tuple-element.13, f32[4]{0:T(128)S(1)} %get-tuple-element.14), channel_id=1, replica_groups=mesh['gz_0'=4,'gz_1'=2,'gz_2'=8,'gx_0'=2,'gx_1'=2] {'gz_1'}, use_global_device_ids=true, to_apply=%region_5.6 | all-reduce | flops 8 | bytes 64 | tf_op jit(solution)/shard_map/psum | solution.py:26
  138.8 10.8 %all-reduce.11 = (f32[4]{0:T(128)S(1)}, f32[4]{0:T(128)S(1)}) all-reduce(f32[4]{0:T(128)S(1)} %get-tuple-element.19, f32[4]{0:T(128)S(1)} %get-tuple-element.20), channel_id=1, replica_groups=mesh['gz_0'=4,'gz_1'=2,'gz_2'=8,'gx_0'=2,'gx_1'=2] {'gz_2'}, use_global_device_ids=true, to_apply=%region_6.7 | all-reduce | flops 8 | bytes 64 | tf_op jit(solution)/shard_map/psum | solution.py:26
  149.6 5.4 %all-reduce.14 = (f32[4]{0:T(128)S(1)}, f32[4]{0:T(128)S(1)}) all-reduce(f32[4]{0:T(128)S(1)} %get-tuple-element.11, f32[4]{0:T(128)S(1)} %get-tuple-element.12), channel_id=1, replica_groups=mesh['gz_0'=4,'gz_1'=2,'gz_2'=8,'gx_0'=2,'gx_1'=2] {'gx_0'}, use_global_device_ids=true, to_apply=%region_7.8 | all-reduce | flops 8 | bytes 64 | tf_op jit(solution)/shard_map/psum | solution.py:26
  155.0 11.8 %all-reduce.13 = (f32[4]{0:T(128)S(1)}, f32[4]{0:T(128)S(1)}) all-reduce(f32[4]{0:T(128)S(1)} %get-tuple-element.17, f32[4]{0:T(128)S(1)} %get-tuple-element.18), channel_id=1, replica_groups=mesh['gz_0'=4,'gz_1'=2,'gz_2'=8,'gx_0'=2,'gx_1'=2] {'gx_1'}, use_global_device_ids=true, to_apply=%region_8.9 | all-reduce | flops 8 | bytes 64 | tf_op jit(solution)/shard_map/psum | solution.py:26
  (96 shorter events, 24.7 us)
Async XLA Ops:
  1.6 9.8 %collective-permute-start = (f32[1,128,512]{2,1,0:T(8,128)S(1)}, f32[1,128,512]{2,1,0:T(8,128)S(1)}, u32[]{:S(2)}, u32[]{:S(2)}) collective-permute-start(f32[1,128,512]{2,1,0:T(8,128)S(1)} %slice.193), channel_id=1, source_target_pairs={{4,0},{8,4},{12,8},{16,12},{20,16},{24,20},{28,24},{32,28},{36,32}... | collective-permute-start | bytes 786440 | tf_op jit(solution)/shard_map/ppermute | solution.py:22
  3.8 7.2 %copy-start = (f32[4,128,512]{2,1,0:T(8,128)S(1)}, f32[4,128,512]{2,1,0:T(8,128)}, u32[]{:S(2)}) copy-start(f32[4,128,512]{2,1,0:T(8,128)} %param.2) | copy-start | bytes 3145732
  3.8 7.6 %collective-permute-start.1 = (f32[4,1,512]{2,1,0:T(1,128)S(1)}, f32[4,1,512]{2,1,0:T(1,128)S(1)}, u32[]{:S(2)}, u32[]{:S(2)}) collective-permute-start(f32[4,1,512]{2,1,0:T(1,128)S(1)} %slice.195), channel_id=1, source_target_pairs={{1,0},{2,1},{3,2},{5,4},{6,5},{7,6},{9,8},{10,9},{11,10},{13,12},{... | collective-permute-start | bytes 24584 | tf_op jit(solution)/shard_map/ppermute | solution.py:22
  11.1 1.2 copy-start.4
  13.8 10.3 %collective-permute-start.2 = (f32[1,128,512]{2,1,0:T(8,128)S(1)}, f32[1,128,512]{2,1,0:T(8,128)S(1)}, u32[]{:S(2)}, u32[]{:S(2)}) collective-permute-start(f32[1,128,512]{2,1,0:T(8,128)S(1)} %slice.254), channel_id=1, source_target_pairs={{0,4},{4,8},{8,12},{12,16},{16,20},{20,24},{24,28},{28,32},{32,36}... | collective-permute-start | bytes 786440 | tf_op jit(solution)/shard_map/ppermute | solution.py:22
  18.1 5.9 %collective-permute-start.3 = (f32[4,1,512]{2,1,0:T(1,128)S(1)}, f32[4,1,512]{2,1,0:T(1,128)S(1)}, u32[]{:S(2)}, u32[]{:S(2)}) collective-permute-start(f32[4,1,512]{2,1,0:T(1,128)S(1)} %slice.256), channel_id=1, source_target_pairs={{0,1},{1,2},{2,3},{4,5},{5,6},{6,7},{8,9},{9,10},{10,11},{12,13},{... | collective-permute-start | bytes 24584 | tf_op jit(solution)/shard_map/ppermute | solution.py:22
  25.1 9.2 %collective-permute-start.4 = (f32[1,128,512]{2,1,0:T(8,128)S(1)}, f32[1,128,512]{2,1,0:T(8,128)S(1)}, u32[]{:S(2)}, u32[]{:S(2)}) collective-permute-start(f32[1,128,512]{2,1,0:T(8,128)S(1)} %slice.260), channel_id=1, source_target_pairs={{4,0},{8,4},{12,8},{16,12},{20,16},{24,20},{28,24},{32,28},{36,32}... | collective-permute-start | bytes 786440 | tf_op jit(solution)/shard_map/ppermute | solution.py:22
  26.4 7.0 %collective-permute-start.5 = (f32[4,1,512]{2,1,0:T(1,128)S(1)}, f32[4,1,512]{2,1,0:T(1,128)S(1)}, u32[]{:S(2)}, u32[]{:S(2)}) collective-permute-start(f32[4,1,512]{2,1,0:T(1,128)S(1)} %slice.262), channel_id=1, source_target_pairs={{1,0},{2,1},{3,2},{5,4},{6,5},{7,6},{9,8},{10,9},{11,10},{13,12},{... | collective-permute-start | bytes 24584 | tf_op jit(solution)/shard_map/ppermute | solution.py:22
  29.0 17.0 %copy-start.1 = (f32[4,128,512]{2,1,0:T(8,128)}, f32[4,128,512]{2,1,0:T(8,128)S(1)}, u32[]{:S(2)}) copy-start(f32[4,128,512]{2,1,0:T(8,128)S(1)} %fusion.72) | copy-start | bytes 3145732
  29.6 16.5 %collective-permute-start.16 = (f32[1,128,512]{2,1,0:T(8,128)S(1)}, f32[1,128,512]{2,1,0:T(8,128)S(1)}, u32[]{:S(2)}, u32[]{:S(2)}) collective-permute-start(f32[1,128,512]{2,1,0:T(8,128)S(1)} %slice.293), channel_id=1, source_target_pairs={{4,0},{8,4},{12,8},{16,12},{20,16},{24,20},{28,24},{32,28},{36,32}... | collective-permute-start | bytes 786440 | tf_op jit(solution)/shard_map/ppermute | solution.py:22
  30.9 15.2 %collective-permute-start.17 = (f32[4,1,512]{2,1,0:T(1,128)S(1)}, f32[4,1,512]{2,1,0:T(1,128)S(1)}, u32[]{:S(2)}, u32[]{:S(2)}) collective-permute-start(f32[4,1,512]{2,1,0:T(1,128)S(1)} %slice.295), channel_id=1, source_target_pairs={{1,0},{2,1},{3,2},{5,4},{6,5},{7,6},{9,8},{10,9},{11,10},{13,12},{... | collective-permute-start | bytes 24584 | tf_op jit(solution)/shard_map/ppermute | solution.py:22
  35.9 10.7 %collective-permute-start.6 = (f32[1,128,512]{2,1,0:T(8,128)S(1)}, f32[1,128,512]{2,1,0:T(8,128)S(1)}, u32[]{:S(2)}, u32[]{:S(2)}) collective-permute-start(f32[1,128,512]{2,1,0:T(8,128)S(1)} %slice.265), channel_id=1, source_target_pairs={{0,4},{4,8},{8,12},{12,16},{16,20},{20,24},{24,28},{28,32},{32,36}... | collective-permute-start | bytes 786440 | tf_op jit(solution)/shard_map/ppermute | solution.py:22
  41.7 4.7 %collective-permute-start.7 = (f32[4,1,512]{2,1,0:T(1,128)S(1)}, f32[4,1,512]{2,1,0:T(1,128)S(1)}, u32[]{:S(2)}, u32[]{:S(2)}) collective-permute-start(f32[4,1,512]{2,1,0:T(1,128)S(1)} %slice.267), channel_id=1, source_target_pairs={{0,1},{1,2},{2,3},{4,5},{5,6},{6,7},{8,9},{9,10},{10,11},{12,13},{... | collective-permute-start | bytes 24584 | tf_op jit(solution)/shard_map/ppermute | solution.py:22
  46.1 1.1 slice-start
  47.2 5.0 %copy-start.2 = (f32[4,128,512]{2,1,0:T(8,128)S(1)}, f32[4,128,512]{2,1,0:T(8,128)}, u32[]{:S(2)}) copy-start(f32[4,128,512]{2,1,0:T(8,128)} %copy-done.1) | copy-start | bytes 3145732
  52.5 9.6 %collective-permute-start.8 = (f32[1,128,512]{2,1,0:T(8,128)S(1)}, f32[1,128,512]{2,1,0:T(8,128)S(1)}, u32[]{:S(2)}, u32[]{:S(2)}) collective-permute-start(f32[1,128,512]{2,1,0:T(8,128)S(1)} %slice.271), channel_id=1, source_target_pairs={{4,0},{8,4},{12,8},{16,12},{20,16},{24,20},{28,24},{32,28},{36,32}... | collective-permute-start | bytes 786440 | tf_op jit(solution)/shard_map/ppermute | solution.py:22
  53.8 6.5 %collective-permute-start.9 = (f32[4,1,512]{2,1,0:T(1,128)S(1)}, f32[4,1,512]{2,1,0:T(1,128)S(1)}, u32[]{:S(2)}, u32[]{:S(2)}) collective-permute-start(f32[4,1,512]{2,1,0:T(1,128)S(1)} %slice.273), channel_id=1, source_target_pairs={{1,0},{2,1},{3,2},{5,4},{6,5},{7,6},{9,8},{10,9},{11,10},{13,12},{... | collective-permute-start | bytes 24584 | tf_op jit(solution)/shard_map/ppermute | solution.py:22
  63.7 13.8 %collective-permute-start.10 = (f32[1,128,512]{2,1,0:T(8,128)S(1)}, f32[1,128,512]{2,1,0:T(8,128)S(1)}, u32[]{:S(2)}, u32[]{:S(2)}) collective-permute-start(f32[1,128,512]{2,1,0:T(8,128)S(1)} %slice.276), channel_id=1, source_target_pairs={{0,4},{4,8},{8,12},{12,16},{16,20},{20,24},{24,28},{28,32},{32,36}... | collective-permute-start | bytes 786440 | tf_op jit(solution)/shard_map/ppermute | solution.py:22
  68.5 9.0 %collective-permute-start.11 = (f32[4,1,512]{2,1,0:T(1,128)S(1)}, f32[4,1,512]{2,1,0:T(1,128)S(1)}, u32[]{:S(2)}, u32[]{:S(2)}) collective-permute-start(f32[4,1,512]{2,1,0:T(1,128)S(1)} %slice.278), channel_id=1, source_target_pairs={{0,1},{1,2},{2,3},{4,5},{5,6},{6,7},{8,9},{9,10},{10,11},{12,13},{... | collective-permute-start | bytes 24584 | tf_op jit(solution)/shard_map/ppermute | solution.py:22
  74.2 27.4 %collective-permute-start.18 = (f32[1,128,512]{2,1,0:T(8,128)S(1)}, f32[1,128,512]{2,1,0:T(8,128)S(1)}, u32[]{:S(2)}, u32[]{:S(2)}) collective-permute-start(f32[1,128,512]{2,1,0:T(8,128)S(1)} %slice.299), channel_id=1, source_target_pairs={{4,0},{8,4},{12,8},{16,12},{20,16},{24,20},{28,24},{32,28},{36,32}... | collective-permute-start | bytes 786440 | tf_op jit(solution)/shard_map/ppermute | solution.py:22
  75.5 21.9 %collective-permute-start.19 = (f32[4,1,512]{2,1,0:T(1,128)S(1)}, f32[4,1,512]{2,1,0:T(1,128)S(1)}, u32[]{:S(2)}, u32[]{:S(2)}) collective-permute-start(f32[4,1,512]{2,1,0:T(1,128)S(1)} %slice.301), channel_id=1, source_target_pairs={{1,0},{2,1},{3,2},{5,4},{6,5},{7,6},{9,8},{10,9},{11,10},{13,12},{... | collective-permute-start | bytes 24584 | tf_op jit(solution)/shard_map/ppermute | solution.py:22
  78.6 11.9 %collective-permute-start.12 = (f32[1,128,512]{2,1,0:T(8,128)S(1)}, f32[1,128,512]{2,1,0:T(8,128)S(1)}, u32[]{:S(2)}, u32[]{:S(2)}) collective-permute-start(f32[1,128,512]{2,1,0:T(8,128)S(1)} %slice.282), channel_id=1, source_target_pairs={{4,0},{8,4},{12,8},{16,12},{20,16},{24,20},{28,24},{32,28},{36,32}... | collective-permute-start | bytes 786440 | tf_op jit(solution)/shard_map/ppermute | solution.py:22
  79.9 6.5 %collective-permute-start.13 = (f32[4,1,512]{2,1,0:T(1,128)S(1)}, f32[4,1,512]{2,1,0:T(1,128)S(1)}, u32[]{:S(2)}, u32[]{:S(2)}) collective-permute-start(f32[4,1,512]{2,1,0:T(1,128)S(1)} %slice.284), channel_id=1, source_target_pairs={{1,0},{2,1},{3,2},{5,4},{6,5},{7,6},{9,8},{10,9},{11,10},{13,12},{... | collective-permute-start | bytes 24584 | tf_op jit(solution)/shard_map/ppermute | solution.py:22
  82.1 19.4 %copy-start.3 = (f32[4,128,512]{2,1,0:T(8,128)}, f32[4,128,512]{2,1,0:T(8,128)S(1)}, u32[]{:S(2)}) copy-start(f32[4,128,512]{2,1,0:T(8,128)S(1)} %fusion.74) | copy-start | bytes 3145732
  82.7 18.9 %collective-permute-start.20 = (f32[1,128,512]{2,1,0:T(8,128)S(1)}, f32[1,128,512]{2,1,0:T(8,128)S(1)}, u32[]{:S(2)}, u32[]{:S(2)}) collective-permute-start(f32[1,128,512]{2,1,0:T(8,128)S(1)} %slice.305), channel_id=1, source_target_pairs={{4,0},{8,4},{12,8},{16,12},{20,16},{24,20},{28,24},{32,28},{36,32}... | collective-permute-start | bytes 786440 | tf_op jit(solution)/shard_map/ppermute | solution.py:22
  86.4 15.2 %collective-permute-start.21 = (f32[4,1,512]{2,1,0:T(1,128)S(1)}, f32[4,1,512]{2,1,0:T(1,128)S(1)}, u32[]{:S(2)}, u32[]{:S(2)}) collective-permute-start(f32[4,1,512]{2,1,0:T(1,128)S(1)} %slice.307), channel_id=1, source_target_pairs={{1,0},{2,1},{3,2},{5,4},{6,5},{7,6},{9,8},{10,9},{11,10},{13,12},{... | collective-permute-start | bytes 24584 | tf_op jit(solution)/shard_map/ppermute | solution.py:22
  92.1 9.7 %collective-permute-start.14 = (f32[1,128,512]{2,1,0:T(8,128)S(1)}, f32[1,128,512]{2,1,0:T(8,128)S(1)}, u32[]{:S(2)}, u32[]{:S(2)}) collective-permute-start(f32[1,128,512]{2,1,0:T(8,128)S(1)} %slice.287), channel_id=1, source_target_pairs={{0,4},{4,8},{8,12},{12,16},{16,20},{20,24},{24,28},{28,32},{32,36}... | collective-permute-start | bytes 786440 | tf_op jit(solution)/shard_map/ppermute | solution.py:22
  97.4 4.4 %collective-permute-start.15 = (f32[4,1,512]{2,1,0:T(1,128)S(1)}, f32[4,1,512]{2,1,0:T(1,128)S(1)}, u32[]{:S(2)}, u32[]{:S(2)}) collective-permute-start(f32[4,1,512]{2,1,0:T(1,128)S(1)} %slice.289), channel_id=1, source_target_pairs={{0,1},{1,2},{2,3},{4,5},{5,6},{6,7},{8,9},{9,10},{10,11},{12,13},{... | collective-permute-start | bytes 24584 | tf_op jit(solution)/shard_map/ppermute | solution.py:22
  101.5 1.1 slice-start.1
where the time goes:
time: 169 us; the launch traced here: 168 us
  starting transfers between devices  65.2 us (39%)
  blocking collectives  53.3 us (32%)
  other arithmetic  29.6 us (18%)
  waiting for transfers between devices  12.4 us (7%)
  local copies, waits for them, and re-layouts  6 us (4%)
    ppermute x22, starting transfers between devices, shifted_2(): lax.ppermute(value, axis, [(source, source + steps) for source in range(i...  65.2 us
    psum x5, blocking collectives, one_axis_at_a_time(): return functools.reduce(lax.psum, axes, array)  53.3 us
    ppermute x22, waiting for transfers between devices, shifted_2(): lax.ppermute(value, axis, [(source, source + steps) for source in range(i...  12.4 us
    reduce_sum x2, other arithmetic, shards(): gap_part = jnp.sum(gap_terms)  10.7 us
    mul x8, other arithmetic, shards(): dual_field = tuple((part * shrink for part in proposed))  6.13 us
    another operation x1, other arithmetic, shards(): jnp.stack(gap_list)  5.06 us
    sub x7, other arithmetic, gradient(): volume[:, :, 1:] - volume[:, :, :-1]  3.94 us
  transfers between devices with their start and end apart: 22, of which 11 were waited for; matrix products, arithmetic and copies ran while one was open for 7% of the time, Pallas kernels for 0%

commit v1 on v0

v1 whole, which is shorter than its diff:
```python
import jax
import jax.numpy as jnp
from jax import lax
from jax.experimental import pallas as pl
from jax.experimental.pallas import tpu as pltpu
from jax.sharding import PartitionSpec as P

ITERS = 4
PRIMAL = 0.28
DUAL = 0.28
TINY = 1.1754944e-38
F32 = jnp.float32
LANES = 128
RING_Z = 8


def spread_rows(ref, planes, row):
    return jnp.concatenate([ref[z, pl.ds(row, 1), :] for z in planes], axis=0)


def lane_next(parts, lane):
    count = len(parts)
    rolled = [pltpu.roll(part, LANES - 1, 1) for part in parts]
    edge = lane == LANES - 1
    return [
        jnp.where(edge, rolled[m + 1] if m + 1 < count else parts[m], rolled[m]) for m in range(count)
    ]


def lane_prev(parts, lane):
    count = len(parts)
    rolled = [pltpu.roll(part, 1, 1) for part in parts]
    edge = lane == 0
    return [
        jnp.where(edge, rolled[m - 1] if m else jnp.zeros_like(parts[0]), rolled[m])
        for m in range(count)
    ]


def cut(value):
    return [value[:, m * LANES : (m + 1) * LANES] for m in range(value.shape[1] // LANES)]


def project(proposed, weight):
    square = proposed[0] * proposed[0] + proposed[1] * proposed[1] + proposed[2] * proposed[2]
    return jnp.minimum(1.0, weight * lax.rsqrt(jnp.maximum(square, TINY)))


def row_dual(here, above, after, dual, weight, keep):
    lane = lax.broadcasted_iota(jnp.int32, (here.shape[0], LANES), 1)
    here, above, after, weight = cut(here), cut(above), cut(after), cut(weight)
    beside = lane_next(here, lane)
    out = []
    for m in range(len(here)):
        delta = ((above[m] - here[m]) * keep, after[m] - here[m], beside[m] - here[m])
        proposed = [DUAL * d for d in delta]
        if dual is not None:
            proposed = [dual[i][m] + proposed[i] for i in range(3)]
        shrink = project(proposed, weight[m])
        out.append([part * shrink for part in proposed])
    return [jnp.concatenate([out[m][i] for m in range(len(here))], axis=1) for i in range(3)]


def make_kernel(planes, rows, cols, n_gz, n_gx):
    blocks = rows // 8
    chunk_rows = 16
    chunks = rows // chunk_rows
    parts = cols // LANES
    cells = planes * rows * cols * n_gz * n_gx
    top = planes
    half = chunks // 2

    def kernel(
        noisy_hbm, weight_hbm, out_ref, gap_ref, step_ref,
        ub, wt, pz, px, py, uu, rx, rdiag, sx, sdiag, swx, wx, prow, totals, slots,
        load_sem, z_send, z_recv, w_send, w_recv, x_send, x_recv, wx_send, wx_recv, r_send, r_recv,
    ):
        gz, gx = lax.axis_index("gz"), lax.axis_index("gx")
        up, down = lax.rem(gz + 1, n_gz), lax.rem(gz + n_gz - 1, n_gz)
        right, left = lax.rem(gx + 1, n_gx), lax.rem(gx + n_gx - 1, n_gx)
        keep_above = jnp.where(gz == n_gz - 1, 0.0, 1.0).astype(F32)
        keep_below = jnp.where(gz == 0, 0.0, 1.0).astype(F32)
        keep_left = jnp.where(gx == 0, 0.0, 1.0).astype(F32)
        at_right = gx == n_gx - 1

        col, z, yh, core = gz // RING_Z, lax.rem(gz, RING_Z), gx // 2, lax.rem(gx, 2)
        first_id = z * 2 + core
        second_id = col * 2 + yh

        def first_peer(i):
            return {"gz": col * RING_Z + i // 2, "gx": yh * 2 + lax.rem(i, 2)}

        def second_peer(i):
            return {"gz": (i // 2) * RING_Z + z, "gx": lax.rem(i, 2) * 2 + core}

        group = 16

        loads = [
            pltpu.make_async_copy(noisy_hbm, ub.at[0, pl.ds(1, planes), pl.ds(0, rows)], load_sem.at[0]),
            pltpu.make_async_copy(weight_hbm, wt.at[pl.ds(1, planes)], load_sem.at[1]),
        ]
        for load in loads:
            load.start()

        barrier = pltpu.get_barrier_semaphore()
        near = [(up, gx), (down, gx), (gz, right), (gz, left), (up, left), (down, right)]
        for a, b in near:
            pl.semaphore_signal(barrier, 1, device_id={"gz": a, "gx": b}, device_id_type=pl.DeviceIdType.MESH)

        def greet(t, carry):
            for own, peer in ((first_id, first_peer), (second_id, second_peer)):
                other = lax.rem(own + t, group)
                pl.semaphore_signal(barrier, 1, device_id=peer(other), device_id_type=pl.DeviceIdType.MESH)
            return carry

        lax.fori_loop(1, group, greet, 0)
        for load in loads:
            load.wait()

        def remote(src, dst, send, recv, a, b):
            return pltpu.make_async_remote_copy(
                src_ref=src, dst_ref=dst, send_sem=send, recv_sem=recv,
                device_id={"gz": a, "gx": b}, device_id_type=pl.DeviceIdType.MESH,
            )

        def chunk_of(c):
            return pl.ds(pl.multiple_of(c * chunk_rows, chunk_rows), chunk_rows)

        def z_up(k, c):
            return remote(ub.at[k, top, chunk_of(c)], ub.at[k, 0, chunk_of(c)],
                          z_send.at[k, 0, c], z_recv.at[k, 0, c], up, gx)

        def z_down(k, c):
            return remote(ub.at[k, 1, chunk_of(c)], ub.at[k, planes + 1, chunk_of(c)],
                          z_send.at[k, 1, c], z_recv.at[k, 1, c], down, gx)

        def w_up(c):
            return remote(wt.at[top, chunk_of(c)], wt.at[0, chunk_of(c)], w_send.at[c], w_recv.at[c], up, gx)

        def x_copy(k, kind):
            if kind == 0:
                return remote(sx.at[k, 0], rx.at[k, 0], x_send.at[k, 0], x_recv.at[k, 0], gz, right)
            if kind == 1:
                return remote(sx.at[k, 1], rx.at[k, 1], x_send.at[k, 1], x_recv.at[k, 1], gz, left)
            if kind == 2:
                return remote(sdiag.at[k, 0], rdiag.at[k, 0], x_send.at[k, 2], x_recv.at[k, 2], down, right)
            return remote(sdiag.at[k, 1], rdiag.at[k, 1], x_send.at[k, 3], x_recv.at[k, 3], up, left)

        def wx_copy():
            return remote(swx, wx, wx_send, wx_recv, gz, right)

        def stage_last_row(k):
            last = spread_rows(ub.at[k], range(1, planes + 1), rows - 1)
            sx[k, 0] = last
            sdiag[k, 0] = last[:1]

        def stage_first_row(k):
            first = spread_rows(ub.at[k], range(1, planes + 1), 0)
            sx[k, 1] = first
            sdiag[k, 1] = first[planes - 1 :]

        stage_last_row(0)
        stage_first_row(0)
        swx[...] = spread_rows(wt, range(1, planes + 1), rows - 1)

        pl.semaphore_wait(barrier, len(near) + 2 * (group - 1))

        def send_first(j, carry):
            c = lax.rem(half - 1 + j, chunks)
            z_up(0, c).start()
            z_down(0, c).start()
            w_up(c).start()
            return carry

        lax.fori_loop(0, chunks, send_first, 0)
        for kind in range(4):
            x_copy(0, kind).start()
        wx_copy().start()

        lane = lax.broadcasted_iota(jnp.int32, (8, LANES), 1)
        sub = lax.broadcasted_iota(jnp.int32, (8, LANES), 0)
        plane_of = lax.broadcasted_iota(jnp.int32, (planes, LANES), 0)
        keep_rows = jnp.where(plane_of == planes - 1, keep_above, 1.0)

        def lanes(m):
            return pl.ds(m * LANES, LANES)

        def first_halo_row(k):
            x_copy(k, 0).wait_recv()
            x_copy(k, 2).wait_recv()
            if k == 0:
                wx_copy().wait_recv()
            here = rx[k, 0]
            above = jnp.concatenate([here[1:], rdiag[k, 0]], axis=0)
            old = None if k == 0 else [cut(prow[i]) for i in range(3)]
            new = row_dual(here, above, sx[k, 1], old, wx[...], keep_rows)
            for i in range(3):
                prow[i] = new[i]
            along = new[1] * keep_left
            for q in range(planes):
                px[k % 2, q + 1, pl.ds(7, 1), :] = along[q : q + 1]

        def last_halo_row(k):
            x_copy(k, 1).wait_recv()
            x_copy(k, 3).wait_recv()
            for q in range(planes + 1):
                row = rx[k, 1, pl.ds(q - 1, 1), :] if q else rdiag[k, 1]
                own = ub[k, q, pl.ds(rows - 1, 1), :]
                row = jnp.where(at_right, own, row)
                ub[k, q, pl.ds(rows, 1), :] = row
                if k and q:
                    before = ub[0, q, pl.ds(rows, 1), :] if k == 1 else uu[(k - 1) % 2, q, pl.ds(rows, 1), :]
                    uu[k % 2, q, pl.ds(rows, 1), :] = 0.5 * (row + before)

        def start_row(k, s):
            own = range(1, planes + 1)
            here = spread_rows(ub.at[k], own, s - 1)
            above = spread_rows(ub.at[k], range(2, planes + 2), s - 1)
            after = spread_rows(ub.at[k], own, s)
            weight = spread_rows(wt, own, s - 1)
            old = None
            if k:
                was = (k - 1) % 2
                old = [
                    cut(spread_rows(pz.at[was], own, s - 1)),
                    cut(spread_rows(px.at[was], own, s - 1 + 8)),
                    cut(spread_rows(py.at[was], own, s - 1)),
                ]
            new = row_dual(here, above, after, old, weight, keep_rows)
            for q in range(planes):
                px[k % 2, q + 1, pl.ds(s - 1 + 8, 1), :] = new[1][q : q + 1]

        def next_rows(block, row):
            return jnp.where(sub == 7, row, pltpu.roll(block, 7, 0))

        def block_step(k, b, sums):
            r = pl.multiple_of(b * 8, 8)
            here_rows, after_row = pl.ds(r, 8), pl.ds(r + 8, 1)
            was, now = (k - 1) % 2, k % 2
            last = k == ITERS - 1

            def get_u(q, m):
                if k == 0:
                    return ub[0, q, here_rows, lanes(m)]
                return uu[now, q, here_rows, lanes(m)]

            if k:
                for m in range(parts):
                    q = planes + 1
                    before = ub[0, q, here_rows, lanes(m)] if k == 1 else uu[was, q, here_rows, lanes(m)]
                    uu[now, q, here_rows, lanes(m)] = 0.5 * (ub[k, q, here_rows, lanes(m)] + before)

            gap_a = gap_b = step_a = jnp.zeros((8, LANES), F32)
            dual_below = None
            for q in range(planes + 1):
                here = [ub[k, q, here_rows, lanes(m)] for m in range(parts)]
                beside = lane_next(here, lane)
                duals, total_var = [], []
                for m in range(parts):
                    delta_z = ub[k, q + 1, here_rows, lanes(m)] - here[m]
                    if q == planes:
                        delta_z = delta_z * keep_above
                    delta_x = next_rows(here[m], ub[k, q, after_row, lanes(m)]) - here[m]
                    delta_y = beside[m] - here[m]
                    weight = wt[q, here_rows, lanes(m)]
                    proposed = [DUAL * delta_z, DUAL * delta_x, DUAL * delta_y]
                    if k:
                        proposed[0] = pz[was, q, here_rows, lanes(m)] + proposed[0]
                        proposed[1] = px[was, q, pl.ds(r + 8, 8), lanes(m)] + proposed[1]
                        proposed[2] = py[was, q, here_rows, lanes(m)] + proposed[2]
                    shrink = project(proposed, weight)
                    new = [part * shrink for part in proposed]
                    if q == 0:
                        new[0] = new[0] * keep_below
                    duals.append(new)
                    if not last:
                        pz[now, q, here_rows, lanes(m)] = new[0]
                        py[now, q, here_rows, lanes(m)] = new[2]
                    if not last or q:
                        px[now, q, pl.ds(r + 8, 8), lanes(m)] = new[1]
                    if k == 0 and q:
                        square = delta_z * delta_z + delta_x * delta_x + delta_y * delta_y
                        total_var.append(weight * (square * lax.rsqrt(jnp.maximum(square, TINY))))
                if q:
                    if k:
                        value = [get_u(q, m) for m in range(parts)]
                        beside_u = lane_next(value, lane)
                        for m in range(parts):
                            delta_z = get_u(q + 1, m) - value[m]
                            if q == planes:
                                delta_z = delta_z * keep_above
                            delta_x = next_rows(value[m], uu[now, q, after_row, lanes(m)]) - value[m]
                            delta_y = beside_u[m] - value[m]
                            square = delta_z * delta_z + delta_x * delta_x + delta_y * delta_y
                            weight = wt[q, here_rows, lanes(m)]
                            total_var.append(weight * (square * lax.rsqrt(jnp.maximum(square, TINY))))
                    else:
                        value = here
                    before_y = lane_prev([d[2] for d in duals], lane)
                    for m in range(parts):
                        above_x = px[now, q, here_rows, lanes(m)]
                        before_x = pltpu.roll(jnp.where(sub == 7, above_x, duals[m][1]), 1, 0)
                        div = (duals[m][0] - dual_below[m]) + (duals[m][1] - before_x) + (duals[m][2] - before_y[m])
                        noisy = ub[0, q, here_rows, lanes(m)]
                        shifted = noisy + div
                        change = (PRIMAL / (1.0 + PRIMAL)) * (shifted - value[m])
                        updated = value[m] + change
                        terms = div * (shifted + noisy)
                        if k:
                            misfit = value[m] - noisy
                            terms = terms + misfit * misfit
                        gap_a = gap_a + terms
                        gap_b = gap_b + total_var[m]
                        step_a = step_a + change * change
                        if last:
                            out_ref[q - 1, here_rows, lanes(m)] = updated
                        else:
                            uu[(k + 1) % 2, q, here_rows, lanes(m)] = updated
                            ub[k + 1, q, here_rows, lanes(m)] = updated + change
                dual_below = [d[0] for d in duals]
            return (sums[0] + (0.5 * gap_a + gap_b), sums[1] + step_a)

        def wait_chunk(k, c):
            z_up(k, c).wait_recv()
            z_down(k, c).wait_recv()
            if k == 0:
                w_up(c).wait_recv()

        for k in range(ITERS):
            first = half + k
            wait_chunk(k, (first - 1) % chunks)
            wait_chunk(k, first % chunks)
            start_row(k, (first % chunks) * chunk_rows)

            def chunk_step(i, sums, k=k, first=first):
                c = lax.rem(first + i, chunks)

                @pl.when(i < chunks - 2)
                def _():
                    wait_chunk(k, lax.rem(c + 1, chunks))

                @pl.when(c == 0)
                def _():
                    first_halo_row(k)

                @pl.when(c == chunks - 1)
                def _():
                    last_halo_row(k)

                sums = lax.fori_loop(0, 2, lambda j, s: block_step(k, 2 * c + j, s), sums)
                if k < ITERS - 1:
                    z_up(k + 1, c).start()
                    z_down(k + 1, c).start()

                    @pl.when(c == 0)
                    def _():
                        stage_first_row(k + 1)
                        x_copy(k + 1, 1).start()
                        x_copy(k + 1, 3).start()

                    @pl.when(c == chunks - 1)
                    def _():
                        stage_last_row(k + 1)
                        x_copy(k + 1, 0).start()
                        x_copy(k + 1, 2).start()

                return sums

            zero = jnp.zeros((8, LANES), F32)
            gap_sum, step_sum = lax.fori_loop(0, chunks, chunk_step, (zero, zero))
            totals[0, pl.ds(k, 1), :] = jnp.sum(gap_sum, axis=0, keepdims=True)
            totals[0, pl.ds(ITERS + k, 1), :] = jnp.sum(step_sum, axis=0, keepdims=True)

        value = totals[0]
        for stage, (own, peer) in enumerate(((first_id, first_peer), (second_id, second_peer))):
            if stage:
                totals[stage] = value
            slots[stage, own] = value

            def r_copy(slot, other, stage=stage, peer=peer):
                return pltpu.make_async_remote_copy(
                    src_ref=totals.at[stage], dst_ref=slots.at[stage, slot],
                    send_sem=r_send.at[stage, other], recv_sem=r_recv.at[stage, slot],
                    device_id=peer(other), device_id_type=pl.DeviceIdType.MESH,
                )

            def send(t, carry, own=own, r_copy=r_copy):
                r_copy(own, lax.rem(own + t, group)).start()
                return carry

            def receive(t, carry, own=own, r_copy=r_copy):
                other = lax.rem(own + t, group)
                r_copy(other, other).wait_recv()
                return carry

            lax.fori_loop(1, group, send, 0)
            lax.fori_loop(1, group, receive, 0)
            value = slots[stage, 0]
            for i in range(1, group):
                value = value + slots[stage, i]

            def sent(t, carry, own=own, r_copy=r_copy):
                r_copy(own, lax.rem(own + t, group)).wait_send()
                return carry

            if stage:
                done = sent
            else:
                done_first = sent

        mean = jnp.sum(value, axis=1, keepdims=True) / cells
        root = jnp.sqrt(mean)
        for k in range(ITERS):
            gap_ref[k] = mean[k, 0]
            step_ref[k] = root[ITERS + k, 0]

        lax.fori_loop(1, group, done_first, 0)
        lax.fori_loop(1, group, done, 0)

        def drain(c, carry):
            for k in range(ITERS):
                z_up(k, c).wait_send()
                z_down(k, c).wait_send()
            w_up(c).wait_send()
            return carry

        lax.fori_loop(0, chunks, drain, 0)
        for k in range(ITERS):
            for kind in range(4):
                x_copy(k, kind).wait_send()
        wx_copy().wait_send()

    return kernel


def solution(mesh):
    n_gz, n_gx = mesh.shape["gz"], mesh.shape["gx"]

    def shards(noisy, weight):
        planes, rows, cols = noisy.shape
        chunks = rows // 16
        dma = pltpu.SemaphoreType.DMA
        return pl.pallas_call(
            make_kernel(planes, rows, cols, n_gz, n_gx),
            name="tv_steps",
            out_shape=(
                jax.ShapeDtypeStruct(noisy.shape, F32),
                jax.ShapeDtypeStruct((ITERS,), F32),
                jax.ShapeDtypeStruct((ITERS,), F32),
            ),
            in_specs=[pl.BlockSpec(memory_space=pl.ANY)] * 2,
            out_specs=(
                pl.BlockSpec(memory_space=pltpu.VMEM),
                pl.BlockSpec(memory_space=pltpu.SMEM),
                pl.BlockSpec(memory_space=pltpu.SMEM),
            ),
            scratch_shapes=[
                pltpu.VMEM((ITERS, planes + 2, rows + 8, cols), F32),
                pltpu.VMEM((planes + 1, rows, cols), F32),
                pltpu.VMEM((2, planes + 1, rows, cols), F32),
                pltpu.VMEM((2, planes + 1, rows + 8, cols), F32),
                pltpu.VMEM((2, planes + 1, rows, cols), F32),
                pltpu.VMEM((2, planes + 2, rows + 8, cols), F32),
                pltpu.VMEM((ITERS, 2, planes, cols), F32),
                pltpu.VMEM((ITERS, 2, 1, cols), F32),
                pltpu.VMEM((ITERS, 2, planes, cols), F32),
                pltpu.VMEM((ITERS, 2, 1, cols), F32),
                pltpu.VMEM((planes, cols), F32),
                pltpu.VMEM((planes, cols), F32),
                pltpu.VMEM((3, planes, cols), F32),
                pltpu.VMEM((2, 8, LANES), F32),
                pltpu.VMEM((2, 16, 8, LANES), F32),
                dma((2,)),
                dma((ITERS, 2, chunks)),
                dma((ITERS, 2, chunks)),
                dma((chunks,)),
                dma((chunks,)),
                dma((ITERS, 4)),
                dma((ITERS, 4)),
                dma,
                dma,
                dma((2, 16)),
                dma((2, 16)),
            ],
            compiler_params=pltpu.CompilerParams(
                collective_id=0, has_side_effects=True, vmem_limit_bytes=60 * 1024 * 1024
            ),
        )(noisy, weight)

    spec = P("gz", "gx", None)
    return jax.shard_map(
        shards, mesh=mesh, in_specs=(spec, spec), out_specs=(spec, P(), P()), check_vma=False
    )
```

time: 169 us -> 68.6 us (0.41)
  starting transfers between devices: 65.2 us -> 0 us
  Pallas kernels: 0 us -> 64.5 us
  blocking collectives: 53.3 us -> 0 us
  other arithmetic: 29.6 us -> 0 us
  waiting for transfers between devices: 12.4 us -> 0 us
  local copies, waits for them, and re-layouts: 6 us -> 3.35 us
    ppermute x22 -> x0, starting transfers between devices: 65.2 us -> none  [shifted_2(): lax.ppermute(value, axis, [(source, source + steps) for source in range(i...]
    pallas_call x0 -> x1, Pallas kernels: none -> 64.5 us  [shards(): pl.pallas_call(make_kernel(planes, rows, cols, n_gz, n_gx), name='tv_step...]
    psum x5 -> x0, blocking collectives: 53.3 us -> none  [one_axis_at_a_time(): return functools.reduce(lax.psum, axes, array)]
    ppermute x22 -> x0, waiting for transfers between devices: 12.4 us -> none  [shifted_2(): lax.ppermute(value, axis, [(source, source + steps) for source in range(i...]
    reduce_sum x2 -> x0, other arithmetic: 10.7 us -> none  [shards(): gap_part = jnp.sum(gap_terms)]
    sub x10 -> x0, other arithmetic: 6.17 us -> none  [the longest x7 3.94 us: gradient(): volume[:, :, 1:] - volume[:, :, :-1]]
    mul x8 -> x0, other arithmetic: 6.13 us -> none  [shards(): dual_field = tuple((part * shrink for part in proposed))]
    slice x42 -> x0, local copies, waits for them, and re-layouts: 5.06 us -> none  [the longest x9 1.78 us: gradient(): volume[1:]]
  transfers between devices with their start and end apart: 22 -> 0, of which waited for: 11 -> 0; matrix products, arithmetic and copies ran while one was open for 7% -> 0% of each run, Pallas kernels for 0% -> 0%
where the time goes in v1:
time: 68.6 us; the launch traced here: 68.5 us
  Pallas kernels  64.5 us (94%)
  local copies, waits for them, and re-layouts  3.35 us (5%)
    pallas_call x1, Pallas kernels, shards(): pl.pallas_call(make_kernel(planes, rows, cols, n_gz, n_gx), name='tv_step...  64.5 us
    unnamed x7, local copies, waits for them, and re-layouts  3.35 us

profile of v1, /device:TPU:1, one launch (start us, length us, event | category | flops | bytes accessed | tf_op | source)
XLA Modules:
  0.0 68.5 jit_solution(17711973334930836092)
XLA Ops:
  0.6 64.5 %tv_steps.1 = (f32[4,128,512]{2,1,0:T(8,128)}, f32[4]{0:T(128)}, f32[4]{0:T(128)}) custom-call(f32[4,128,512]{2,1,0:T(8,128)} %noisy_hbm.1, f32[4,128,512]{2,1,0:T(8,128)} %weight_hbm.1), custom_call_target="tpu_custom_call" | custom-call | tf_op jit(solution)/shard_map/tv_steps/pallas_call | solution.py:443
  65.1 0.0 copy-start.1
  65.1 2.3 %copy.8 = f32[4,128,512]{2,1,0:T(8,128)} copy(f32[4,128,512]{2,1,0:T(8,128)} %get-tuple-element.6) | data formatting | bytes 2097152
  67.4 0.0 copy-done.1
  67.4 0.0 copy-start
  67.4 0.5 copy.9
  67.9 0.1 copy-done
  68.0 0.5 copy.10
Async XLA Ops:
  65.1 2.3 %copy-start.1 = (f32[4]{0:T(128)S(1)}, f32[4]{0:T(128)}, u32[]{:S(2)}) copy-start(f32[4]{0:T(128)} %get-tuple-element.7) | copy-start | bytes 52
  67.4 0.6 copy-start

commit v2 on v0

v2 whole, which is shorter than its diff:
```python
import jax
import jax.numpy as jnp
from jax import lax
from jax.experimental import pallas as pl
from jax.experimental.pallas import tpu as pltpu
from jax.sharding import PartitionSpec as P

ITERS = 4
PRIMAL = 0.28
DUAL = 0.28
TINY = 1.1754944e-38
F32 = jnp.float32
LANES = 128
RING_Z = 8
GROUP = 16
EXT = 8
BLOCK = 8
CHUNK = 16
MESH = pl.DeviceIdType.MESH


def lane_next(parts, lane):
    count = len(parts)
    rolled = [pltpu.roll(part, LANES - 1, 1) for part in parts]
    edge = lane == LANES - 1
    return [
        jnp.where(edge, rolled[m + 1] if m + 1 < count else parts[m], rolled[m]) for m in range(count)
    ]


def lane_prev(parts, lane):
    count = len(parts)
    rolled = [pltpu.roll(part, 1, 1) for part in parts]
    edge = lane == 0
    return [
        jnp.where(edge, rolled[m - 1] if m else jnp.zeros_like(parts[0]), rolled[m])
        for m in range(count)
    ]


def root_inverse(square):
    return lax.rsqrt(jnp.maximum(square, TINY))


def norm2(vector):
    return vector[0] * vector[0] + vector[1] * vector[1] + vector[2] * vector[2]


def make_kernel(planes, rows, cols, n_gz, n_gx):
    parts = cols // LANES
    cells = planes * rows * cols * n_gz * n_gx
    top = planes
    blocks = (rows + 2 * EXT) // BLOCK
    chunks = blocks * BLOCK // CHUNK
    own_first, own_last = 1, blocks - 2

    def kernel(
        noisy_hbm, weight_hbm, out_ref, sums_ref,
        ub, wt, pz, py, uu, px, edges, beside, totals, slots,
        load_sem, z_send, z_recv, w_send, w_recv, x_send, x_recv, r_send, r_recv,
    ):
        gz, gx = lax.axis_index("gz"), lax.axis_index("gx")
        up, down = lax.rem(gz + 1, n_gz), lax.rem(gz + n_gz - 1, n_gz)
        right, left = lax.rem(gx + 1, n_gx), lax.rem(gx + n_gx - 1, n_gx)
        keep_above = jnp.where(gz == n_gz - 1, 0.0, 1.0).astype(F32)
        keep_below = jnp.where(gz == 0, 0.0, 1.0).astype(F32)
        keep_left = jnp.where(gx == 0, 0.0, 1.0).astype(F32)
        keep_right = jnp.where(gx == n_gx - 1, 0.0, 1.0).astype(F32)

        col, z, yh, core = gz // RING_Z, lax.rem(gz, RING_Z), gx // 2, lax.rem(gx, 2)
        first_id = z * 2 + core
        second_id = col * 2 + yh

        def first_peer(i):
            return {"gz": col * RING_Z + i // 2, "gx": yh * 2 + lax.rem(i, 2)}

        def second_peer(i):
            return {"gz": (i // 2) * RING_Z + z, "gx": lax.rem(i, 2) * 2 + core}

        loads = [
            pltpu.make_async_copy(src.at[:, :, pl.ds(m * LANES, LANES)],
                                  dst.at[pl.ds(1, planes), m, pl.ds(EXT, rows)], load_sem.at[i, m])
            for i, (src, dst) in enumerate(((noisy_hbm, ub.at[0]), (weight_hbm, wt)))
            for m in range(parts)
        ]
        for load in loads:
            load.start()

        barrier = pltpu.get_barrier_semaphore()
        near = [(up, gx), (down, gx), (gz, right), (gz, left)]
        for a, b in near:
            pl.semaphore_signal(barrier, 1, device_id={"gz": a, "gx": b}, device_id_type=MESH)

        def greet(t, carry):
            for own, peer in ((first_id, first_peer), (second_id, second_peer)):
                pl.semaphore_signal(barrier, 1, device_id=peer(lax.rem(own + t, GROUP)), device_id_type=MESH)
            return carry

        lax.fori_loop(1, GROUP, greet, 0)
        for load in loads:
            load.wait()

        def remote(src, dst, send, recv, a, b):
            return pltpu.make_async_remote_copy(
                src_ref=src, dst_ref=dst, send_sem=send, recv_sem=recv,
                device_id={"gz": a, "gx": b}, device_id_type=MESH,
            )

        def chunk_rows(k, c):
            if isinstance(c, int) and c in (0, chunks - 1):
                margin = ITERS - k
                if c == 0:
                    return pl.ds(EXT - margin, CHUNK - EXT + margin)
                return pl.ds(c * CHUNK, CHUNK - EXT + margin)
            return pl.ds(pl.multiple_of(c * CHUNK, CHUNK), CHUNK)

        def z_up(k, c):
            at = chunk_rows(k, c)
            return remote(ub.at[k, top, :, at], ub.at[k, 0, :, at], z_send.at[k, 0, c], z_recv.at[k, 0, c], up, gx)

        def z_down(k, c):
            at = chunk_rows(k, c)
            return remote(ub.at[k, 1, :, at], ub.at[k, top + 1, :, at], z_send.at[k, 1, c], z_recv.at[k, 1, c], down, gx)

        def w_up(c):
            at = chunk_rows(0, c)
            return remote(wt.at[top, :, at], wt.at[0, :, at], w_send.at[c], w_recv.at[c], up, gx)

        own_planes = pl.ds(1, planes)
        arrays = (ub.at[0, own_planes], wt.at[own_planes])
        x_copies = []
        for i, (source, to, side) in enumerate(((EXT + rows - ITERS, EXT - ITERS, right), (EXT, EXT + rows, left))):
            for n, array in enumerate(arrays):
                edges[i, n] = array[:, :, pl.ds(source, ITERS), :]
                x_copies.append(remote(edges.at[i, n], beside.at[i, n], x_send.at[i, n], x_recv.at[i, n], gz, side))

        pl.semaphore_wait(barrier, len(near) + 2 * (GROUP - 1))
        for copy in x_copies:
            copy.start()

        def receive_x(i):
            to = (EXT - ITERS, EXT + rows)[i]
            for n, array in enumerate(arrays):
                x_copies[2 * i + n].wait_recv()
                array[:, :, pl.ds(to, ITERS), :] = beside[i, n]

        def send_first(c):
            z_up(0, c).start()
            w_up(c).start()
            z_down(0, c).start()

        def send_loop(c, carry):
            send_first(c)
            return carry

        for copy in x_copies:
            copy.wait_send()
        receive_x(0)
        send_first(0)
        receive_x(1)
        lax.fori_loop(1, chunks - 1, send_loop, 0)
        send_first(chunks - 1)

        lane = lax.broadcasted_iota(jnp.int32, (BLOCK, LANES), 1)
        sub = lax.broadcasted_iota(jnp.int32, (BLOCK, LANES), 0)
        keep_last_row = jnp.where(sub == BLOCK - 1, keep_right, 1.0)

        def get_u(k, q, m, at):
            return ub[0, q, m, at, :] if k == 0 else uu[k % 2, q, m, at, :]

        def block_step(k, j, sums, place="own"):
            r = j * BLOCK if isinstance(j, int) else pl.multiple_of(j * BLOCK, BLOCK)
            at, at_next = pl.ds(r, BLOCK), pl.ds(r + 1, BLOCK)
            at_x, at_before_x = pl.ds(r + BLOCK, BLOCK), pl.ds(r + BLOCK - 1, BLOCK)
            was, now = (k - 1) % 2, k % 2
            last = k == ITERS - 1
            counted = place in ("own", "last")
            update = counted or not last

            if k:
                for m in range(parts):
                    new = (0.5 / DUAL) * ub[k, top + 1, m, at, :] + 0.5 * get_u(k - 1, top + 1, m, at)
                    uu[now, top + 1, m, at, :] = new

            gap_a = gap_b = step_a = jnp.zeros((BLOCK, LANES), F32)
            dual_below = None
            for q in range(planes + 1):
                here = [ub[k, q, m, at, :] for m in range(parts)]
                beside = lane_next(here, lane)
                duals, total_var = [], []
                for m in range(parts):
                    delta = [ub[k, q + 1, m, at, :] - here[m], ub[k, q, m, at_next, :] - here[m], beside[m] - here[m]]
                    if q == top:
                        delta[0] = delta[0] * keep_above
                    if place == "last":
                        delta[1] = delta[1] * keep_last_row
                    weight = wt[q, m, at, :]
                    if k:
                        proposed = [
                            pz[was, q, m, at, :] + delta[0],
                            px[was, q, m, at_x, :] + delta[1],
                            py[was, q, m, at, :] + delta[2],
                        ]
                    else:
                        proposed = [DUAL * part for part in delta]
                    shrink = jnp.minimum(1.0, weight * root_inverse(norm2(proposed)))
                    new = [part * shrink for part in proposed]
                    if q == 0:
                        new[0] = new[0] * keep_below
                    if place == "first":
                        new[1] = new[1] * keep_left
                    duals.append(new)
                    if not last:
                        pz[now, q, m, at, :] = new[0]
                        py[now, q, m, at, :] = new[2]
                    if not last or q:
                        px[now, q, m, at_x, :] = new[1]
                    if k == 0 and q and counted:
                        square = norm2(delta)
                        total_var.append(weight * (square * root_inverse(square)))
                if q and update:
                    value = here if k == 0 else [get_u(k, q, m, at) for m in range(parts)]
                    if k and counted:
                        beside_u = lane_next(value, lane)
                        for m in range(parts):
                            delta = [
                                get_u(k, q + 1, m, at) - value[m],
                                get_u(k, q, m, at_next) - value[m],
                                beside_u[m] - value[m],
                            ]
                            if q == top:
                                delta[0] = delta[0] * keep_above
                            if place == "last":
                                delta[1] = delta[1] * keep_last_row
                            square = norm2(delta)
                            total_var.append(wt[q, m, at, :] * (square * root_inverse(square)))
                    before_y = lane_prev([d[2] for d in duals], lane)
                    for m in range(parts):
                        before_x = px[now, q, m, at_before_x, :]
                        div = (duals[m][0] - dual_below[m]) + (duals[m][1] - before_x) + (duals[m][2] - before_y[m])
                        noisy = ub[0, q, m, at, :]
                        shifted = noisy + div
                        change = (PRIMAL / (1.0 + PRIMAL)) * (shifted - value[m])
                        updated = value[m] + change
                        if counted:
                            terms = div * (shifted + noisy)
                            if k:
                                misfit = value[m] - noisy
                                terms = terms + misfit * misfit
                            gap_a = gap_a + terms
                            gap_b = gap_b + total_var[m]
                            step_a = step_a + change * change
                        if last:
                            out_ref[q - 1, pl.ds(r - EXT, BLOCK), pl.ds(m * LANES, LANES)] = updated
                        else:
                            uu[(k + 1) % 2, q, m, at, :] = updated
                            ub[k + 1, q, m, at, :] = DUAL * (updated + change)
                dual_below = [d[0] for d in duals]
            if not counted:
                return sums
            return (sums[0] + (0.5 * gap_a + gap_b), sums[1] + step_a)

        def send_chunk(k, c):
            if k < ITERS - 1:
                z_up(k + 1, c).start()
                z_down(k + 1, c).start()

        def wait_up(k, c):
            z_up(k, c).wait_recv()
            if k == 0:
                w_up(c).wait_recv()

        for k in range(ITERS):
            zero = jnp.zeros((BLOCK, LANES), F32)
            sums = (zero, zero)
            wait_up(k, 0)
            z_down(k, 0).wait_recv()
            wait_up(k, 1)
            sums = block_step(k, 0, sums, "first")
            sums = block_step(k, 1, sums)
            send_chunk(k, 0)

            def chunk_step(c, sums, k=k):
                z_down(k, c).wait_recv()

                @pl.when(c < chunks - 2)
                def _():
                    wait_up(k, c + 1)

                @pl.when(c == chunks - 2)
                def _():
                    wait_up(k, chunks - 1)

                sums = lax.fori_loop(0, CHUNK // BLOCK, lambda i, s: block_step(k, 2 * c + i, s), sums)
                send_chunk(k, c)
                return sums

            sums = lax.fori_loop(1, chunks - 1, chunk_step, sums)
            z_down(k, chunks - 1).wait_recv()
            sums = block_step(k, own_last, sums, "last")
            if k < ITERS - 1:
                block_step(k, own_last + 1, sums, "after")
            send_chunk(k, chunks - 1)
            totals[0, pl.ds(k, 1), :] = jnp.sum(sums[0], axis=0, keepdims=True)
            totals[0, pl.ds(ITERS + k, 1), :] = jnp.sum(sums[1], axis=0, keepdims=True)

        by_row = jnp.sum(totals[0], axis=1, keepdims=True)
        value = jnp.sum(jnp.where(lane == sub, by_row, 0.0), axis=0, keepdims=True)
        done = []
        for stage, (mine, peer) in enumerate(((first_id, first_peer), (second_id, second_peer))):
            slots[stage, mine] = value
            totals[1 + stage, pl.ds(0, 1), :] = value

            def r_copy(slot, other, stage=stage, peer=peer):
                return pltpu.make_async_remote_copy(
                    src_ref=totals.at[1 + stage, pl.ds(0, 1)], dst_ref=slots.at[stage, slot],
                    send_sem=r_send.at[stage, other], recv_sem=r_recv.at[stage, slot],
                    device_id=peer(other), device_id_type=MESH,
                )

            def send(t, carry, mine=mine, r_copy=r_copy):
                r_copy(mine, lax.rem(mine + t, GROUP)).start()
                return carry

            def receive(t, carry, mine=mine, r_copy=r_copy):
                other = lax.rem(mine + t, GROUP)
                r_copy(other, other).wait_recv()
                return carry

            def sent(t, carry, mine=mine, r_copy=r_copy):
                r_copy(mine, lax.rem(mine + t, GROUP)).wait_send()
                return carry

            lax.fori_loop(1, GROUP, send, 0)
            lax.fori_loop(1, GROUP, receive, 0)
            value = slots[stage, 0]
            for i in range(1, GROUP):
                value = value + slots[stage, i]
            done.append(sent)

        mean = value / cells
        sums_ref[...] = jnp.where(lane[:1] < ITERS, mean, jnp.sqrt(mean))

        for sent in done:
            lax.fori_loop(1, GROUP, sent, 0)

        def drain(c):
            for k in range(ITERS):
                z_up(k, c).wait_send()
                z_down(k, c).wait_send()
            w_up(c).wait_send()

        def drain_loop(c, carry):
            drain(c)
            return carry

        drain(0)
        lax.fori_loop(1, chunks - 1, drain_loop, 0)
        drain(chunks - 1)

    return kernel


def solution(mesh):
    n_gz, n_gx = mesh.shape["gz"], mesh.shape["gx"]

    def shards(noisy, weight):
        planes, rows, cols = noisy.shape
        parts = cols // LANES
        chunks = (rows + 2 * EXT) // CHUNK
        tall = rows + 3 * EXT
        dma = pltpu.SemaphoreType.DMA
        denoised, sums = pl.pallas_call(
            make_kernel(planes, rows, cols, n_gz, n_gx),
            name="tv_steps",
            out_shape=(
                pltpu.VMEM(noisy.shape, F32),
                pltpu.VMEM((1, LANES), F32),
            ),
            in_specs=[pl.BlockSpec(memory_space=pl.ANY)] * 2,
            out_specs=(
                pl.BlockSpec(memory_space=pltpu.VMEM),
                pl.BlockSpec(memory_space=pltpu.VMEM),
            ),
            scratch_shapes=[
                pltpu.VMEM((ITERS, planes + 2, parts, tall, LANES), F32),
                pltpu.VMEM((planes + 1, parts, tall, LANES), F32),
                pltpu.VMEM((2, planes + 1, parts, tall, LANES), F32),
                pltpu.VMEM((2, planes + 1, parts, tall, LANES), F32),
                pltpu.VMEM((2, planes + 2, parts, tall, LANES), F32),
                pltpu.VMEM((2, planes + 1, parts, tall + 2 * EXT, LANES), F32),
                pltpu.VMEM((2, 2, planes, parts, ITERS, LANES), F32),
                pltpu.VMEM((2, 2, planes, parts, ITERS, LANES), F32),
                pltpu.VMEM((3, 8, LANES), F32),
                pltpu.VMEM((2, GROUP, 1, LANES), F32),
                dma((2, parts)),
                dma((ITERS, 2, chunks)),
                dma((ITERS, 2, chunks)),
                dma((chunks,)),
                dma((chunks,)),
                dma((2, 2)),
                dma((2, 2)),
                dma((2, GROUP)),
                dma((2, GROUP)),
            ],
            compiler_params=pltpu.CompilerParams(
                collective_id=0, has_side_effects=True, vmem_limit_bytes=60 * 1024 * 1024
            ),
        )(noisy, weight)
        return denoised, sums[0, :ITERS], sums[0, ITERS : 2 * ITERS]

    spec = P("gz", "gx", None)
    return jax.shard_map(
        shards, mesh=mesh, in_specs=(spec, spec), out_specs=(spec, P(), P()), check_vma=False
    )
```

time: 169 us -> 60.1 us (0.36)
  starting transfers between devices: 65.2 us -> 0 us
  Pallas kernels: 0 us -> 57.7 us
  blocking collectives: 53.3 us -> 0 us
  other arithmetic: 29.6 us -> 0 us
  waiting for transfers between devices: 12.4 us -> 0 us
  local copies, waits for them, and re-layouts: 6 us -> 1.55 us
    ppermute x22 -> x0, starting transfers between devices: 65.2 us -> none  [shifted_2(): lax.ppermute(value, axis, [(source, source + steps) for source in range(i...]
    pallas_call x0 -> x1, Pallas kernels: none -> 57.7 us  [shards(): pl.pallas_call(make_kernel(planes, rows, cols, n_gz, n_gx), name='tv_step...]
    psum x5 -> x0, blocking collectives: 53.3 us -> none  [one_axis_at_a_time(): return functools.reduce(lax.psum, axes, array)]
    ppermute x22 -> x0, waiting for transfers between devices: 12.4 us -> none  [shifted_2(): lax.ppermute(value, axis, [(source, source + steps) for source in range(i...]
    reduce_sum x2 -> x0, other arithmetic: 10.7 us -> none  [shards(): gap_part = jnp.sum(gap_terms)]
    sub x10 -> x0, other arithmetic: 6.17 us -> none  [the longest x7 3.94 us: gradient(): volume[:, :, 1:] - volume[:, :, :-1]]
    mul x8 -> x0, other arithmetic: 6.13 us -> none  [shards(): dual_field = tuple((part * shrink for part in proposed))]
    slice x42 -> x0, local copies, waits for them, and re-layouts: 5.06 us -> none  [the longest x9 1.78 us: gradient(): volume[1:]]
  transfers between devices with their start and end apart: 22 -> 0, of which waited for: 11 -> 0; matrix products, arithmetic and copies ran while one was open for 7% -> 0% of each run, Pallas kernels for 0% -> 0%
where the time goes in v2:
time: 60.1 us; the launch traced here: 59.9 us
  Pallas kernels  57.7 us (96%)
  local copies, waits for them, and re-layouts  1.55 us (3%)
  between operations  0.64 us (1%)
    pallas_call x1, Pallas kernels, shards(): pl.pallas_call(make_kernel(planes, rows, cols, n_gz, n_gx), name='tv_step...  57.7 us

profile of v2, /device:TPU:1, one launch (start us, length us, event | category | flops | bytes accessed | tf_op | source)
XLA Modules:
  0.0 59.9 jit_solution(2658451560140064328)
XLA Ops:
  0.6 57.7 %tv_steps.1 = (f32[4,128,512]{2,1,0:T(8,128)S(1)}, f32[1,128]{1,0:T(1,128)S(1)}) custom-call(f32[4,128,512]{2,1,0:T(8,128)} %noisy_hbm.1, f32[4,128,512]{2,1,0:T(8,128)} %weight_hbm.1), custom_call_target="tpu_custom_call" | custom-call | tf_op jit(solution)/shard_map/tv_steps/pallas_call | solution.py:373
  58.4 1.0 %copy.6 = f32[4,128,512]{2,1,0:T(8,128)} copy(f32[4,128,512]{2,1,0:T(8,128)S(1)} %get-tuple-element.9) | data formatting | bytes 2097152
  59.4 0.6 slice_bitcast_fusion

commit v3 on v2

--- a/solution.py
+++ b/solution.py
@@ -155,10 +155,11 @@
 
         for copy in x_copies:
             copy.wait_send()
+        send_first(1)
         receive_x(0)
         send_first(0)
         receive_x(1)
-        lax.fori_loop(1, chunks - 1, send_loop, 0)
+        lax.fori_loop(2, chunks - 1, send_loop, 0)
         send_first(chunks - 1)
 
         lane = lax.broadcasted_iota(jnp.int32, (BLOCK, LANES), 1)
@@ -304,9 +305,23 @@
             totals[0, pl.ds(k, 1), :] = jnp.sum(sums[0], axis=0, keepdims=True)
             totals[0, pl.ds(ITERS + k, 1), :] = jnp.sum(sums[1], axis=0, keepdims=True)
 
+        def drain(c):
+            for k in range(ITERS):
+                z_up(k, c).wait_send()
+                z_down(k, c).wait_send()
+            w_up(c).wait_send()
+
+        def drain_loop(c, carry):
+            drain(c)
+            return carry
+
+        def drain_all():
+            drain(0)
+            lax.fori_loop(1, chunks - 1, drain_loop, 0)
+            drain(chunks - 1)
+
         by_row = jnp.sum(totals[0], axis=1, keepdims=True)
         value = jnp.sum(jnp.where(lane == sub, by_row, 0.0), axis=0, keepdims=True)
-        done = []
         for stage, (mine, peer) in enumerate(((first_id, first_peer), (second_id, second_peer))):
             slots[stage, mine] = value
             totals[1 + stage, pl.ds(0, 1), :] = value
@@ -331,32 +346,18 @@
                 r_copy(mine, lax.rem(mine + t, GROUP)).wait_send()
                 return carry
 
-            lax.fori_loop(1, GROUP, send, 0)
+            for t in range(1, GROUP):
+                send(t, 0)
+            if stage == 0:
+                drain_all()
+            lax.fori_loop(1, GROUP, sent, 0)
             lax.fori_loop(1, GROUP, receive, 0)
             value = slots[stage, 0]
             for i in range(1, GROUP):
                 value = value + slots[stage, i]
-            done.append(sent)
 
         mean = value / cells
         sums_ref[...] = jnp.where(lane[:1] < ITERS, mean, jnp.sqrt(mean))
-
-        for sent in done:
-            lax.fori_loop(1, GROUP, sent, 0)
-
-        def drain(c):
-            for k in range(ITERS):
-                z_up(k, c).wait_send()
-                z_down(k, c).wait_send()
-            w_up(c).wait_send()
-
-        def drain_loop(c, carry):
-            drain(c)
-            return carry
-
-        drain(0)
-        lax.fori_loop(1, chunks - 1, drain_loop, 0)
-        drain(chunks - 1)
 
     return kernel
 

time: 60.1 us -> 58.3 us (0.970)
  Pallas kernels: 57.7 us -> 56 us
    pallas_call x1, Pallas kernels: 57.7 us -> 56 us  [shards(): pl.pallas_call(make_kernel(planes, rows, cols, n_gz, n_gx), name='tv_step...]
where the time goes in v3:
time: 58.3 us; the launch traced here: 58.2 us
  Pallas kernels  56 us (96%)
  local copies, waits for them, and re-layouts  1.55 us (3%)
  between operations  0.64 us (1%)
    pallas_call x1, Pallas kernels, shards(): pl.pallas_call(make_kernel(planes, rows, cols, n_gz, n_gx), name='tv_step...  56 us

profile of v3, /device:TPU:1, one launch (start us, length us, event | category | flops | bytes accessed | tf_op | source)
XLA Modules:
  0.0 58.2 jit_solution(16416260148469075130)
XLA Ops:
  0.6 56.0 %tv_steps.1 = (f32[4,128,512]{2,1,0:T(8,128)S(1)}, f32[1,128]{1,0:T(1,128)S(1)}) custom-call(f32[4,128,512]{2,1,0:T(8,128)} %noisy_hbm.1, f32[4,128,512]{2,1,0:T(8,128)} %weight_hbm.1), custom_call_target="tpu_custom_call" | custom-call | tf_op jit(solution)/shard_map/tv_steps/pallas_call | solution.py:374
  56.6 1.0 %copy.6 = f32[4,128,512]{2,1,0:T(8,128)} copy(f32[4,128,512]{2,1,0:T(8,128)S(1)} %get-tuple-element.9) | data formatting | bytes 2097152
  57.6 0.6 %slice_bitcast_fusion = (f32[4]{0:T(128)}, f32[4]{0:T(128)}) fusion(f32[1,128]{1,0:T(1,128)S(1)} %get-tuple-element.6), kind=kLoop, calls=%fused_computation | loop fusion | bytes 64 | tf_op jit(solution)/shard_map/squeeze | solution.py:411

commit v4 on v3

--- a/solution.py
+++ b/solution.py
@@ -16,6 +16,7 @@
 EXT = 8
 BLOCK = 8
 CHUNK = 16
+EARLY = 16
 MESH = pl.DeviceIdType.MESH
 
 
@@ -52,7 +53,9 @@
     top = planes
     blocks = (rows + 2 * EXT) // BLOCK
     chunks = blocks * BLOCK // CHUNK
-    own_first, own_last = 1, blocks - 2
+    own_last = blocks - 2
+    per_chunk = CHUNK // BLOCK
+    inner_end = own_last // per_chunk
 
     def kernel(
         noisy_hbm, weight_hbm, out_ref, sums_ref,
@@ -132,7 +135,7 @@
         for i, (source, to, side) in enumerate(((EXT + rows - ITERS, EXT - ITERS, right), (EXT, EXT + rows, left))):
             for n, array in enumerate(arrays):
                 edges[i, n] = array[:, :, pl.ds(source, ITERS), :]
-                x_copies.append(remote(edges.at[i, n], beside.at[i, n], x_send.at[i, n], x_recv.at[i, n], gz, side))
+            x_copies.append(remote(edges.at[i], beside.at[i], x_send.at[i], x_recv.at[i], gz, side))
 
         pl.semaphore_wait(barrier, len(near) + 2 * (GROUP - 1))
         for copy in x_copies:
@@ -140,8 +143,8 @@
 
         def receive_x(i):
             to = (EXT - ITERS, EXT + rows)[i]
+            x_copies[i].wait_recv()
             for n, array in enumerate(arrays):
-                x_copies[2 * i + n].wait_recv()
                 array[:, :, pl.ds(to, ITERS), :] = beside[i, n]
 
         def send_first(c):
@@ -155,11 +158,12 @@
 
         for copy in x_copies:
             copy.wait_send()
-        send_first(1)
+        early = jnp.where(jnp.logical_or(z == 0, z == RING_Z - 1), 1, 3)
+        lax.fori_loop(1, 1 + early, send_loop, 0)
         receive_x(0)
         send_first(0)
         receive_x(1)
-        lax.fori_loop(2, chunks - 1, send_loop, 0)
+        lax.fori_loop(1 + early, chunks - 1, send_loop, 0)
         send_first(chunks - 1)
 
         lane = lax.broadcasted_iota(jnp.int32, (BLOCK, LANES), 1)
@@ -274,34 +278,40 @@
         for k in range(ITERS):
             zero = jnp.zeros((BLOCK, LANES), F32)
             sums = (zero, zero)
-            wait_up(k, 0)
-            z_down(k, 0).wait_recv()
-            wait_up(k, 1)
-            sums = block_step(k, 0, sums, "first")
-            sums = block_step(k, 1, sums)
-            send_chunk(k, 0)
+            def edge_chunk(c, sums, k=k):
+                z_down(k, c).wait_recv()
+                if c + 1 < chunks:
+                    wait_up(k, c + 1)
+                for j in range(c * per_chunk, (c + 1) * per_chunk):
+                    place = {0: "first", own_last: "last", own_last + 1: "after"}.get(j, "own")
+                    if place != "after" or k < ITERS - 1:
+                        sums = block_step(k, j, sums, place)
+                send_chunk(k, c)
+                return sums
 
             def chunk_step(c, sums, k=k):
                 z_down(k, c).wait_recv()
 
-                @pl.when(c < chunks - 2)
+                @pl.when(c < inner_end - 1)
                 def _():
                     wait_up(k, c + 1)
 
-                @pl.when(c == chunks - 2)
+                @pl.when(c == inner_end - 1)
                 def _():
-                    wait_up(k, chunks - 1)
-
-                sums = lax.fori_loop(0, CHUNK // BLOCK, lambda i, s: block_step(k, 2 * c + i, s), sums)
+                    wait_up(k, inner_end)
+
+                if per_chunk == 1:
+                    sums = block_step(k, c, sums)
+                else:
+                    sums = lax.fori_loop(0, per_chunk, lambda i, s: block_step(k, per_chunk * c + i, s), sums)
                 send_chunk(k, c)
                 return sums
 
-            sums = lax.fori_loop(1, chunks - 1, chunk_step, sums)
-            z_down(k, chunks - 1).wait_recv()
-            sums = block_step(k, own_last, sums, "last")
-            if k < ITERS - 1:
-                block_step(k, own_last + 1, sums, "after")
-            send_chunk(k, chunks - 1)
+            wait_up(k, 0)
+            sums = edge_chunk(0, sums)
+            sums = lax.fori_loop(1, inner_end, chunk_step, sums)
+            for c in range(inner_end, chunks):
+                sums = edge_chunk(c, sums)
             totals[0, pl.ds(k, 1), :] = jnp.sum(sums[0], axis=0, keepdims=True)
             totals[0, pl.ds(ITERS + k, 1), :] = jnp.sum(sums[1], axis=0, keepdims=True)
 
@@ -399,8 +409,8 @@
                 dma((ITERS, 2, chunks)),
                 dma((chunks,)),
                 dma((chunks,)),
-                dma((2, 2)),
-                dma((2, 2)),
+                dma((2,)),
+                dma((2,)),
                 dma((2, GROUP)),
                 dma((2, GROUP)),
             ],

time: 58.3 us -> 58.3 us (level)
  no operation moved by 1% of the time
where the time goes in v4:
time: 58.3 us; the launch traced here: 58.1 us
  Pallas kernels  55.9 us (96%)
  local copies, waits for them, and re-layouts  1.55 us (3%)
  between operations  0.64 us (1%)
    pallas_call x1, Pallas kernels, shards(): pl.pallas_call(make_kernel(planes, rows, cols, n_gz, n_gx), name='tv_step...  55.9 us

profile of v4, /device:TPU:1, one launch (start us, length us, event | category | flops | bytes accessed | tf_op | source)
XLA Modules:
  0.0 58.1 jit_solution(8514643388624596254)
XLA Ops:
  0.6 55.9 %tv_steps.1 = (f32[4,128,512]{2,1,0:T(8,128)S(1)}, f32[1,128]{1,0:T(1,128)S(1)}) custom-call(f32[4,128,512]{2,1,0:T(8,128)} %noisy_hbm.1, f32[4,128,512]{2,1,0:T(8,128)} %weight_hbm.1), custom_call_target="tpu_custom_call" | custom-call | tf_op jit(solution)/shard_map/tv_steps/pallas_call | solution.py:384
  56.6 1.0 %copy.6 = f32[4,128,512]{2,1,0:T(8,128)} copy(f32[4,128,512]{2,1,0:T(8,128)S(1)} %get-tuple-element.9) | data formatting | bytes 2097152
  57.6 0.6 %slice_bitcast_fusion = (f32[4]{0:T(128)}, f32[4]{0:T(128)}) fusion(f32[1,128]{1,0:T(1,128)S(1)} %get-tuple-element.6), kind=kLoop, calls=%fused_computation | loop fusion | bytes 64 | tf_op jit(solution)/shard_map/squeeze | solution.py:421
